TPU v7x, 32 devices: a whole 2x2x4 slice. The times are simulated.
32 devices in a mesh: region: 8 (over z, y), sub: 4 (over x, core).
Axes of the slice: x: 2, y: 2, z: 4, core: 2. Of those that a mesh axis runs over, the one named last changes fastest.
Arguments:
- density: bfloat16 [8, 4, 192, 2048], P('region', 'sub'), may hold values from -6 to 6
- inverse: bfloat16 [8, 4, 2048, 2048], P('region', 'sub'), may hold values from -0.125 to 0.125
- projection: bfloat16 [8, 4, 2048, 256], P('region', 'sub'), may hold values from -0.125 to 0.125
- points: float32 [8, 4, 3, 2048], P('region'), may hold values from 0 to 1
- skeleton_points: float32 [8, 4, 3, 256], replicated, may hold values from 0 to 1
- neighbours: int32 [8, 4, 2], P('region', 'sub'), may hold values from 0 to 3, as said below
- reads: int32 [8, 16, 2], replicated, may hold values from 0 to 7, as said below
Outputs:
- result: bfloat16 [8, 4, 192, 2048], P('region', 'sub')
Inputs may be any that keep to these rules, and one draw needn't show every extreme that they name: `neighbours`: each subdomain lists 2 distinct other subdomains of its own region. In reads[g], entries c * 4 to (c + 1) * 4 - 1 have block index // 2 equal to c; their owner regions are distinct and differ from g.
All inputs are finite; a program needn't handle non-finite values.
Results may differ from a plain program's by a relative error of at most 0.0067.
Values may be sent and summed in bfloat16 or wider, within the bound.
A program may use at most 128 MiB of HBM per device.

v0:
```python
import jax
import jax.numpy as jnp
from jax import lax
from jax.sharding import PartitionSpec as P

BLOCK_ROWS = 128
damping = 1.0
softening = 0.05


def kernel(source, target):
    apart_x = source[0][:, None] - target[0][None, :]
    apart_y = source[1][:, None] - target[1][None, :]
    apart_z = source[2][:, None] - target[2][None, :]
    squared = apart_x * apart_x + apart_y * apart_y + apart_z * apart_z
    kernel_tiles = jnp.exp(-damping * jnp.sqrt(squared)) / jnp.sqrt(squared + softening * softening)
    return (kernel_tiles * target.shape[1] ** (-0.5)).astype(jnp.bfloat16)


def per_device(density, inverse, projection, points, skeleton_points, neighbours, reads):
    sub_index = lax.axis_index("sub")
    region_index = lax.axis_index("region")
    groups = lax.axis_size("sub")
    local_rhs = density[0, 0]
    block_inverse = inverse[0, 0]
    rows_rhs = local_rhs.shape[0]
    solved = jnp.dot(local_rhs, block_inverse, preferred_element_type=jnp.float32).astype(
        jnp.bfloat16
    )
    strengths = jnp.dot(solved, projection[0, 0], preferred_element_type=jnp.float32).astype(
        jnp.bfloat16
    )
    region_points = points[0]
    own_points = lax.dynamic_index_in_dim(region_points, sub_index, 0, keepdims=False)
    listed = neighbours[0, 0]
    zeros_field = jnp.zeros(solved.shape, jnp.float32)
    shards = lax.all_gather(solved[None], "sub", axis=0, tiled=True)

    def add_one(offset, running):
        source = lax.dynamic_index_in_dim(shards, offset, 0, keepdims=False)
        mate_points = lax.dynamic_index_in_dim(region_points, offset, 0, keepdims=False)

        def evaluate(total):
            return total + jnp.dot(
                source, kernel(mate_points, own_points), preferred_element_type=jnp.float32
            )

        def unchanged(total):
            return total

        return lax.cond(jnp.any(listed == offset), evaluate, unchanged, running)

    near_field = lax.fori_loop(0, shards.shape[0], add_one, zeros_field)
    block_rows = BLOCK_ROWS
    blocks_each = strengths.shape[1] // block_rows
    per_column = reads.shape[1] // groups
    my_reads = lax.dynamic_index_in_dim(reads, region_index, 0, keepdims=False)
    column_reads = lax.dynamic_slice_in_dim(my_reads, sub_index * per_column, per_column, 0)
    owners = column_reads[:, 0]
    wanted = lax.dynamic_slice_in_dim(reads, sub_index * per_column, per_column, 1)
    matches = wanted[:, :, 0] == region_index
    present = jnp.any(matches, axis=1)
    halves = jnp.sum(jnp.where(matches, wanted[:, :, 1] % blocks_each, 0), axis=1)
    split_blocks = jnp.transpose(strengths.reshape(rows_rhs, blocks_each, block_rows), (1, 0, 2))
    outgoing = jnp.where(
        present[:, None, None], jnp.take(split_blocks, halves, axis=0), jnp.zeros((), jnp.bfloat16)
    )
    arrived = lax.all_to_all(outgoing, "region", split_axis=0, concat_axis=0, tiled=True)
    picked = jnp.take(arrived, owners, axis=0)
    add_shards = lax.all_gather(picked, "sub", axis=0, tiled=True)
    count_rows = add_shards.shape[0]
    group_size = 4

    def add_group(offset, running):
        first_row = offset * group_size
        entries = lax.dynamic_slice_in_dim(my_reads, first_row, group_size, 0)
        group_owners = entries[:, 0]
        group_columns = entries[:, 1] // blocks_each
        group_halves = entries[:, 1] % blocks_each
        located = skeleton_points[group_owners, group_columns].reshape(
            group_size, 3, blocks_each, block_rows
        )
        located = jnp.take_along_axis(located, group_halves[:, None, None, None], axis=2)[:, :, 0]
        sources = jnp.transpose(located, (1, 0, 2)).reshape(3, group_size * block_rows)
        values = lax.dynamic_slice_in_dim(add_shards, first_row, group_size, 0)
        values = jnp.transpose(values, (1, 0, 2)).reshape(rows_rhs, group_size * block_rows)
        return running + jnp.dot(
            values, kernel(sources, own_points), preferred_element_type=jnp.float32
        )

    far_field = lax.fori_loop(0, count_rows // group_size, add_group, zeros_field)
    applied = (local_rhs.astype(jnp.float32) + near_field + far_field).astype(jnp.bfloat16)
    result = jnp.dot(applied, block_inverse, preferred_element_type=jnp.float32).astype(
        jnp.bfloat16
    )
    return result[None, None]


def solution(mesh):
    return jax.shard_map(
        per_device,
        mesh=mesh,
        in_specs=(
            P("region", "sub", None, None),
            P("region", "sub", None, None),
            P("region", "sub", None, None),
            P("region", None, None, None),
            P(),
            P("region", "sub", None),
            P(),
        ),
        out_specs=P("region", "sub", None, None),
        check_vma=False,
    )
```

profile of v0, /device:TPU:0, one launch (start us, length us, event | category | flops | bytes accessed | tf_op | source)
XLA Modules:
  0.0 123.5 jit_solution(12675178542980507038)
XLA Ops:
  6.5 6.4 %fusion.33 = bf16[192,2048]{1,0:T(8,128)(2,1)} fusion(bf16[1,1,2048,2048]{3,2,1,0:T(8,128)(2,1)} %param.14, bf16[1,1,192,2048]{3,2,1,0:T(8,128)(2,1)} %param.13), kind=kOutput, calls=%fused_computation.63 | convolution fusion | flops 1611005952 | bytes 9961472 | tf_op jit(solution)/shard_map/dot_general | solution.py:27
  13.6 1.5 %fusion.42 = bf16[24,2,8,128]{3,2,1,0:T(8,128)(2,1)S(1)} fusion(bf16[192,2048]{1,0:T(8,128)(2,1)} %fusion.33, bf16[1,1,2048,256]{3,2,1,0:T(8,128)(2,1)S(1)} %copy-done), kind=kOutput, calls=%fused_computation.68 | convolution fusion | flops 201375744 | bytes 1933312 | tf_op jit(solution)/shard_map/dot_general | solution.py:30
  15.2 0.6 gather_fusion.2
  15.8 0.9 select_select_fusion
  16.7 7.3 %all-to-all-start = ((bf16[8,192,128]{2,1,0:T(8,128)(2,1)}), bf16[8,192,128]{2,1,0:T(8,128)(2,1)S(1)}, u32[]{:S(2)}, u32[]{:S(2)}) async-start(bf16[8,192,128]{2,1,0:T(8,128)(2,1)} %select_select_fusion), calls=%async_computation | async-start | bytes 786432 | tf_op jit(solution)/shard_map/all_to_all | solution.py:68
  24.1 0.7 copy.47
  24.8 0.7 copy.33
  25.6 10.1 %all-to-all-done = bf16[8,192,128]{2,1,0:T(8,128)(2,1)S(1)} async-done(((bf16[8,192,128]{2,1,0:T(8,128)(2,1)}), bf16[8,192,128]{2,1,0:T(8,128)(2,1)S(1)}, u32[]{:S(2)}, u32[]{:S(2)}) %all-to-all-start) | async-done | bytes 393248 | tf_op jit(solution)/shard_map/all_to_all | solution.py:68
  35.7 0.6 gather_fusion.3
  36.4 11.5 %all_gather.7 = bf16[16,192,128]{2,1,0:T(8,128)(2,1)S(1)} all-gather(bf16[4,192,128]{2,1,0:T(8,128)(2,1)S(1)} %broadcast_select_fusion), channel_id=1, replica_groups=mesh['region'=8,'sub'=4] {'sub'}, dimensions={0}, use_global_device_ids=true | all-gather | bytes 983040 | tf_op jit(solution)/shard_map/all_gather | solution.py:70
  47.9 24.9 %while.33 = (s32[]{:T(128)}, f32[192,2048]{1,0:T(8,128)S(1)}, bf16[16,192,128]{2,1,0:T(8,128)(2,1)S(1)}, s32[16,2]{0,1:T(2,128)S(1)}, f32[8,4,3,256]{3,2,1,0:T(4...) while((s32[]{:T(128)}, f32[192,2048]{1,0:T(8,128)S(1)}, ...), condition=%wide.region_8.9_spmd.clone, body=%wide.region_7.8_spmd.clone.sunk | while | flops 417072896 | bytes 4319797 | solution.py:91
  48.0 1.5 %gather_fusion = f32[4,3,256]{2,1,0:T(4,128)S(1)} fusion(f32[8,4,3,256]{3,2,1,0:T(4,128)} %get-tuple-element.545, s32[4]{0:T(128)S(1)} %get-tuple-element.513), kind=kCustom, calls=%fused_computation.clone.clone.1 | custom fusion | bytes 24608 | tf_op jit(solution)/shard_map/while/body/eval_jaxpr/gather | solution.py:80
  50.4 3.7 %convolution_add_fusion.2 = f32[192,2048]{1,0:T(8,128)S(1)} fusion(f32[2048]{0:T(1024)S(1)} %bitcast.130, f32[512]{0:T(512)S(1)} %bitcast.136, f32[2048]{0:T(1024)S(1)} %bitcast.131, f32[512]{0:T(512)S(1)} %bitcast.137, f32[2048]{0:T(1024)S(1)} %bitcast.129, f32[512]{0:T(512)S(1)} %bitcast.135, f32[192,2048]{1,0:T(8,128)S(1)} %get-tuple-element.532, ...), kind=kOutput, calls=%fused_computation.18.clone.1 | convolution fusion | flops 417071104 | bytes 3373057 | tf_op jit(solution)/shard_map/while/body/eval_jaxpr/dot_general | solution.py:87
  54.3 1.5 %gather_fusion = f32[4,3,256]{2,1,0:T(4,128)S(1)} fusion(f32[8,4,3,256]{3,2,1,0:T(4,128)} %get-tuple-element.545, s32[4]{0:T(128)S(1)} %get-tuple-element.513), kind=kCustom, calls=%fused_computation.clone.clone.1 | custom fusion | bytes 24608 | tf_op jit(solution)/shard_map/while/body/eval_jaxpr/gather | solution.py:80
  56.7 3.7 %convolution_add_fusion.2 = f32[192,2048]{1,0:T(8,128)S(1)} fusion(f32[2048]{0:T(1024)S(1)} %bitcast.130, f32[512]{0:T(512)S(1)} %bitcast.136, f32[2048]{0:T(1024)S(1)} %bitcast.131, f32[512]{0:T(512)S(1)} %bitcast.137, f32[2048]{0:T(1024)S(1)} %bitcast.129, f32[512]{0:T(512)S(1)} %bitcast.135, f32[192,2048]{1,0:T(8,128)S(1)} %get-tuple-element.532, ...), kind=kOutput, calls=%fused_computation.18.clone.1 | convolution fusion | flops 417071104 | bytes 3373057 | tf_op jit(solution)/shard_map/while/body/eval_jaxpr/dot_general | solution.py:87
  60.5 1.5 %gather_fusion = f32[4,3,256]{2,1,0:T(4,128)S(1)} fusion(f32[8,4,3,256]{3,2,1,0:T(4,128)} %get-tuple-element.545, s32[4]{0:T(128)S(1)} %get-tuple-element.513), kind=kCustom, calls=%fused_computation.clone.clone.1 | custom fusion | bytes 24608 | tf_op jit(solution)/shard_map/while/body/eval_jaxpr/gather | solution.py:80
  62.9 3.7 %convolution_add_fusion.2 = f32[192,2048]{1,0:T(8,128)S(1)} fusion(f32[2048]{0:T(1024)S(1)} %bitcast.130, f32[512]{0:T(512)S(1)} %bitcast.136, f32[2048]{0:T(1024)S(1)} %bitcast.131, f32[512]{0:T(512)S(1)} %bitcast.137, f32[2048]{0:T(1024)S(1)} %bitcast.129, f32[512]{0:T(512)S(1)} %bitcast.135, f32[192,2048]{1,0:T(8,128)S(1)} %get-tuple-element.532, ...), kind=kOutput, calls=%fused_computation.18.clone.1 | convolution fusion | flops 417071104 | bytes 3373057 | tf_op jit(solution)/shard_map/while/body/eval_jaxpr/dot_general | solution.py:87
  66.8 1.5 %gather_fusion = f32[4,3,256]{2,1,0:T(4,128)S(1)} fusion(f32[8,4,3,256]{3,2,1,0:T(4,128)} %get-tuple-element.545, s32[4]{0:T(128)S(1)} %get-tuple-element.513), kind=kCustom, calls=%fused_computation.clone.clone.1 | custom fusion | bytes 24608 | tf_op jit(solution)/shard_map/while/body/eval_jaxpr/gather | solution.py:80
  69.2 3.7 %convolution_add_fusion.2 = f32[192,2048]{1,0:T(8,128)S(1)} fusion(f32[2048]{0:T(1024)S(1)} %bitcast.130, f32[512]{0:T(512)S(1)} %bitcast.136, f32[2048]{0:T(1024)S(1)} %bitcast.131, f32[512]{0:T(512)S(1)} %bitcast.137, f32[2048]{0:T(1024)S(1)} %bitcast.129, f32[512]{0:T(512)S(1)} %bitcast.135, f32[192,2048]{1,0:T(8,128)S(1)} %get-tuple-element.532, ...), kind=kOutput, calls=%fused_computation.18.clone.1 | convolution fusion | flops 417071104 | bytes 3373057 | tf_op jit(solution)/shard_map/while/body/eval_jaxpr/dot_general | solution.py:87
  72.9 1.1 copy-done.1
  74.2 35.9 %while.32 = (s32[]{:T(128)}, f32[192,2048]{1,0:T(8,128)S(1)}, s32[2]{0:T(128)S(1)}, bf16[4,192,2048]{2,1,0:T(8,128)(2,1)}, f32[4,3,2048]{2,1,0:T(4,128)}, /*index=5*/f32[3,2048]{1,0:T(4,128)S(1)}, s32[]{:T(128)}) while((s32[]{:T(128)}, f32[192,2048]{1,0:T(8,128)S(1)}, s32[2]{0:T(128)S(1)}, bf16[4,192,2048]{2,1,0:T(8,128)(2,1)}, ...), condition=%wide.region_4.5_spmd, body=%wide.region_0.4_spmd.sunk | while | flops 1665531904 | bytes 4080315 | solution.py:53
  74.4 0.7 compare_reduce_fusion.2
  75.7 0.7 compare_reduce_fusion.2
  77.0 15.2 %conditional.2 = (f32[192,2048]{1,0:T(8,128)S(1)}) conditional(s32[]{:T(128)} %convert_element_type.63, f32[192,2048]{1,0:T(8,128)S(1)} %get-tuple-element.559, (s32[]{:T(128)}, bf16[4,192,2048]{2,1,0:T(8,128)(2,1)}, f32[4,3,2048]{2,1,0:T(4,128)}, f32[3,2048]{1,0:T(4,128)S(1)}, f32[192,2048]{1,0:T(8,128)S(1)}) %tuple.98), branch_computations={%region_2.2_spmd, %region_3.3_spmd} | conditional | flops 1665531904 | bytes 4080172 | solution.py:51
  77.0 0.9 constant_dynamic-slice_fusion.1
  77.9 14.3 %fusion.1 = f32[192,2048]{1,0:T(8,128)S(1)} fusion(f32[192,2048]{1,0:T(8,128)S(1)} %get-tuple-element.323, f32[2048]{0:T(1024)S(1)} %bitcast.133, f32[2048]{0:T(1024)S(1)} %bitcast.128, f32[2048]{0:T(1024)S(1)} %bitcast.134, f32[2048]{0:T(1024)S(1)} %bitcast.127, f32[2048]{0:T(1024)S(1)} %bitcast.132, f32[2048]{0:T(1024)S(1)} %bitcast.126, ...), kind=kOutput, calls=%fused_computation.6 | convolution fusion | flops 1665531904 | bytes 3981824 | tf_op jit(solution)/shard_map/while/body/eval_jaxpr/cond/branch_1_fun/dot_general | solution.py:44
  92.2 0.7 compare_reduce_fusion.2
  93.5 15.2 %conditional.2 = (f32[192,2048]{1,0:T(8,128)S(1)}) conditional(s32[]{:T(128)} %convert_element_type.63, f32[192,2048]{1,0:T(8,128)S(1)} %get-tuple-element.559, (s32[]{:T(128)}, bf16[4,192,2048]{2,1,0:T(8,128)(2,1)}, f32[4,3,2048]{2,1,0:T(4,128)}, f32[3,2048]{1,0:T(4,128)S(1)}, f32[192,2048]{1,0:T(8,128)S(1)}) %tuple.98), branch_computations={%region_2.2_spmd, %region_3.3_spmd} | conditional | flops 1665531904 | bytes 4080172 | solution.py:51
  93.5 0.9 constant_dynamic-slice_fusion.1
  94.5 14.3 %fusion.1 = f32[192,2048]{1,0:T(8,128)S(1)} fusion(f32[192,2048]{1,0:T(8,128)S(1)} %get-tuple-element.323, f32[2048]{0:T(1024)S(1)} %bitcast.133, f32[2048]{0:T(1024)S(1)} %bitcast.128, f32[2048]{0:T(1024)S(1)} %bitcast.134, f32[2048]{0:T(1024)S(1)} %bitcast.127, f32[2048]{0:T(1024)S(1)} %bitcast.132, f32[2048]{0:T(1024)S(1)} %bitcast.126, ...), kind=kOutput, calls=%fused_computation.6 | convolution fusion | flops 1665531904 | bytes 3981824 | tf_op jit(solution)/shard_map/while/body/eval_jaxpr/cond/branch_1_fun/dot_general | solution.py:44
  108.8 0.7 compare_reduce_fusion.2
  110.1 6.6 %fusion.39 = bf16[1,1,192,2048]{3,2,1,0:T(8,128)(2,1)} fusion(bf16[1,1,2048,2048]{3,2,1,0:T(8,128)(2,1)} %param.14, f32[192,2048]{1,0:T(8,128)} %copy-done.1, f32[192,2048]{1,0:T(8,128)S(1)} %get-tuple-element.344, bf16[1,1,192,2048]{3,2,1,0:T(8,128)(2,1)S(1)} %copy-done.2), kind=kOutput, calls=%fused_computation.65 | convolution fusion | flops 1612578816 | bytes 13107200 | tf_op jit(solution)/shard_map/dot_general | solution.py:93
  (95 shorter events, 5.2 us)
Async XLA Ops:
  6.5 7.1 %copy-start = (bf16[1,1,2048,256]{3,2,1,0:T(8,128)(2,1)S(1)}, bf16[1,1,2048,256]{3,2,1,0:T(8,128)(2,1)}, u32[]{:S(2)}) copy-start(bf16[1,1,2048,256]{3,2,1,0:T(8,128)(2,1)} %param.15) | copy-start | bytes 3145732
  6.5 6.4 %copy-start.5 = (s32[8,16,2]{1,2,0:T(2,128)S(1)}, s32[8,16,2]{1,2,0:T(2,128)}, u32[]{:S(2)}) copy-start(s32[8,16,2]{1,2,0:T(2,128)} %param.19) | copy-start | bytes 3076
  6.5 66.3 %all-gather.3.cloned.1.call-start = ((), (), s32[]{:S(2)}) async-start(), calls=%async_computation.1 | async-start | bytes 3932160 | tf_op jit(solution)/shard_map/all_gather | solution.py:37
  12.9 11.1 %copy-start.3 = (f32[1,4,3,2048]{3,1,2,0:T(4,128)S(1)}, f32[1,4,3,2048]{3,1,2,0:T(4,128)}, u32[]{:S(2)}) copy-start(f32[1,4,3,2048]{3,1,2,0:T(4,128)} %param.16) | copy-start | bytes 294916
  12.9 11.9 %copy-start.4 = (f32[8,4,3,256]{3,1,2,0:T(4,128)S(1)}, f32[8,4,3,256]{3,1,2,0:T(4,128)}, u32[]{:S(2)}) copy-start(f32[8,4,3,256]{3,1,2,0:T(4,128)} %param.17) | copy-start | bytes 294916
  16.7 19.0 %all-to-all-start = ((bf16[8,192,128]{2,1,0:T(8,128)(2,1)}), bf16[8,192,128]{2,1,0:T(8,128)(2,1)S(1)}, u32[]{:S(2)}, u32[]{:S(2)}) async-start(bf16[8,192,128]{2,1,0:T(8,128)(2,1)} %select_select_fusion), calls=%async_computation | async-start | bytes 786432 | tf_op jit(solution)/shard_map/all_to_all | solution.py:68
  47.9 26.3 %copy-start.6 = (s32[1,1,2]{2,1,0:T(1,128)S(1)}, s32[1,1,2]{2,1,0:T(1,128)}, u32[]{:S(2)}) copy-start(s32[1,1,2]{2,1,0:T(1,128)} %param.18) | copy-start | bytes 28
  72.8 1.2 copy-start.1
  74.2 35.9 %copy-start.2 = (bf16[1,1,192,2048]{3,2,1,0:T(8,128)(2,1)S(1)}, bf16[1,1,192,2048]{3,2,1,0:T(8,128)(2,1)}, u32[]{:S(2)}) copy-start(bf16[1,1,192,2048]{3,2,1,0:T(8,128)(2,1)} %param.13) | copy-start | bytes 2359300
Sparse Core Ops, SparseCore 0:
  13.1 34.1 all-gather.2
where the time goes:
time: 124 us
  matrix products  57.7 us (47%)
  local copies, waits for them, and re-layouts  15.6 us (13%)
  between operations  13.6 us (11%)
  blocking collectives  11.5 us (9%)
  waiting for transfers between devices  10.1 us (8%)
  starting transfers between devices  7.31 us (6%)
  other arithmetic  4.52 us (4%)
  loops' own time  3.2 us (3%)
    dot_general x2, matrix products, evaluate(): jnp.dot(source, kernel(mate_points, own_points), preferred_element_type=j...  28.5 us
    dot_general x4, matrix products, add_group(): jnp.dot(values, kernel(sources, own_points), preferred_element_type=jnp.f...  14.7 us
    all_gather x1, blocking collectives, per_device(): add_shards = lax.all_gather(picked, 'sub', axis=0, tiled=True)  11.5 us
    all_to_all x1, waiting for transfers between devices, per_device(): lax.all_to_all(outgoing, 'region', split_axis=0, concat_axis=0, tiled=True)  10.1 us
    all_to_all x1, starting transfers between devices, per_device(): lax.all_to_all(outgoing, 'region', split_axis=0, concat_axis=0, tiled=True)  7.31 us
    dot_general x1, matrix products, per_device(): jnp.dot(applied, block_inverse, preferred_element_type=jnp.float32)  6.56 us
    dot_general x1, matrix products, per_device(): jnp.dot(local_rhs, block_inverse, preferred_element_type=jnp.float32)  6.4 us
    gather x8, local copies, waits for them, and re-layouts, add_group(): skeleton_points[group_owners, group_columns]  5.96 us
  transfers between devices with their start and end apart: 2, of which 1 were waited for; matrix products, arithmetic and copies ran while one was open for 25% of the time, Pallas kernels for 0%

commit v1 on v0

--- a/solution.py
+++ b/solution.py
@@ -6,6 +6,17 @@
 BLOCK_ROWS = 128
 damping = 1.0
 softening = 0.05
+
+
+def turned_line(value, axis, d):
+    devices = lax.axis_size(axis)
+    route = [(i, (i + 1) % devices) for i in range(devices)]
+    blocks = [value]
+    for stride in range(1, devices):
+        blocks = [lax.ppermute(blocks[0], axis, route), *blocks]
+    whole = jnp.concatenate(blocks, axis=d)
+    offset = (lax.axis_index(axis) + 1) * blocks[-1].shape[d]
+    return jnp.roll(whole, offset, axis=d)
 
 
 def kernel(source, target):
@@ -67,7 +78,7 @@
     )
     arrived = lax.all_to_all(outgoing, "region", split_axis=0, concat_axis=0, tiled=True)
     picked = jnp.take(arrived, owners, axis=0)
-    add_shards = lax.all_gather(picked, "sub", axis=0, tiled=True)
+    add_shards = turned_line(picked, "sub", 0)
     count_rows = add_shards.shape[0]
     group_size = 4
 

time: 124 us -> 130 us (1.048); the launches traced: 124 us -> 128 us
  waiting for transfers between devices: 10.1 us -> 23.6 us
  blocking collectives: 11.5 us -> 0 us
  local copies, waits for them, and re-layouts: 15.6 us -> 19.3 us
  matrix products: 57.7 us -> 55.6 us
    ppermute x0 -> x3, waiting for transfers between devices: none -> 12.7 us  [turned_line(): blocks = [lax.ppermute(blocks[0], axis, route), *blocks]]
    all_gather x1 -> x0, blocking collectives: 11.5 us -> none  [per_device(): add_shards = lax.all_gather(picked, 'sub', axis=0, tiled=True)]
    unnamed x17 -> x23, local copies, waits for them, and re-layouts: 2.58 us -> 3.48 us
  transfers between devices with their start and end apart: 2 -> 5, of which waited for: 1 -> 4; matrix products, arithmetic and copies ran while one was open for 25% -> 23% of each run, Pallas kernels for 0% -> 0%
where the time goes in v1:
time: 130 us; the launch traced here: 128 us
  matrix products  55.6 us (43%)
  waiting for transfers between devices  23.6 us (18%)
  local copies, waits for them, and re-layouts  19.3 us (15%)
  between operations  13.7 us (11%)
  starting transfers between devices  7.41 us (6%)
  other arithmetic  5.5 us (4%)
  loops' own time  3.14 us (2%)
    dot_general x2, matrix products, evaluate(): jnp.dot(source, kernel(mate_points, own_points), preferred_element_type=j...  28.5 us
    dot_general x4, matrix products, add_group(): jnp.dot(values, kernel(sources, own_points), preferred_element_type=jnp.f...  14.7 us
    ppermute x3, waiting for transfers between devices, turned_line(): blocks = [lax.ppermute(blocks[0], axis, route), *blocks]  12.7 us
    all_to_all x1, waiting for transfers between devices, per_device(): lax.all_to_all(outgoing, 'region', split_axis=0, concat_axis=0, tiled=True)  10.8 us
    all_to_all x1, starting transfers between devices, per_device(): lax.all_to_all(outgoing, 'region', split_axis=0, concat_axis=0, tiled=True)  7.31 us
    dot_general x1, matrix products, per_device(): jnp.dot(applied, block_inverse, preferred_element_type=jnp.float32)  6.56 us
    gather x8, local copies, waits for them, and re-layouts, add_group(): skeleton_points[group_owners, group_columns]  5.96 us
    dot_general x1, matrix products, per_device(): jnp.dot(local_rhs, block_inverse, preferred_element_type=jnp.float32)  5.44 us
  transfers between devices with their start and end apart: 5, of which 4 were waited for; matrix products, arithmetic and copies ran while one was open for 23% of the time, Pallas kernels for 0%

profile of v1, /device:TPU:0, one launch (start us, length us, event | category | flops | bytes accessed | tf_op | source)
XLA Modules:
  0.0 128.2 jit_solution(9125630569446282959)
XLA Ops:
  6.5 0.9 constant_dynamic-slice_fusion.7
  7.5 1.0 fusion.53
  8.7 5.4 %fusion.33 = bf16[192,2048]{1,0:T(8,128)(2,1)S(1)} fusion(bf16[1,1,2048,2048]{3,2,1,0:T(8,128)(2,1)} %param.14, bf16[1,1,192,2048]{3,2,1,0:T(8,128)(2,1)} %param.13), kind=kOutput, calls=%fused_computation.63 | convolution fusion | flops 1611005952 | bytes 9961472 | tf_op jit(solution)/shard_map/dot_general | solution.py:38
  15.2 0.9 select_select_fusion
  16.1 7.3 %all-to-all-start = ((bf16[8,192,128]{2,1,0:T(8,128)(2,1)}), bf16[8,192,128]{2,1,0:T(8,128)(2,1)S(1)}, u32[]{:S(2)}, u32[]{:S(2)}) async-start(bf16[8,192,128]{2,1,0:T(8,128)(2,1)} %select_select_fusion), calls=%async_computation | async-start | bytes 786432 | tf_op jit(solution)/shard_map/all_to_all | solution.py:79
  23.4 0.8 fusion.49
  24.2 10.8 %all-to-all-done = bf16[8,192,128]{2,1,0:T(8,128)(2,1)S(1)} async-done(((bf16[8,192,128]{2,1,0:T(8,128)(2,1)}), bf16[8,192,128]{2,1,0:T(8,128)(2,1)S(1)}, u32[]{:S(2)}, u32[]{:S(2)}) %all-to-all-start) | async-done | bytes 393248 | tf_op jit(solution)/shard_map/all_to_all | solution.py:79
  35.8 5.1 %collective-permute-done = bf16[4,192,128]{2,1,0:T(8,128)(2,1)S(1)} collective-permute-done((bf16[4,192,128]{2,1,0:T(8,128)(2,1)S(1)}, bf16[4,192,128]{2,1,0:T(8,128)(2,1)S(1)}, u32[]{:S(2)}, u32[]{:S(2)}) %collective-permute-start) | collective-permute-done | bytes 196640 | tf_op jit(solution)/shard_map/ppermute | solution.py:16
  40.9 5.1 %collective-permute-done.1 = bf16[4,192,128]{2,1,0:T(8,128)(2,1)S(1)} collective-permute-done((bf16[4,192,128]{2,1,0:T(8,128)(2,1)S(1)}, bf16[4,192,128]{2,1,0:T(8,128)(2,1)S(1)}, u32[]{:S(2)}, u32[]{:S(2)}) %collective-permute-start.1) | collective-permute-done | bytes 196640 | tf_op jit(solution)/shard_map/ppermute | solution.py:16
  46.6 0.7 copy.39
  47.3 0.8 copy.41
  48.1 0.7 copy.25
  48.8 0.7 fusion.50
  49.5 2.6 %collective-permute-done.2 = bf16[4,192,128]{2,1,0:T(8,128)(2,1)S(1)} collective-permute-done((bf16[4,192,128]{2,1,0:T(8,128)(2,1)S(1)}, bf16[4,192,128]{2,1,0:T(8,128)(2,1)S(1)}, u32[]{:S(2)}, u32[]{:S(2)}) %collective-permute-start.2) | collective-permute-done | bytes 196640 | tf_op jit(solution)/shard_map/ppermute | solution.py:16
  52.6 25.0 %while.33 = (s32[]{:T(128)}, f32[192,2048]{1,0:T(8,128)S(1)}, bf16[16,192,128]{2,1,0:T(8,128)(2,1)S(1)}, s32[16,2]{0,1:T(2,128)S(1)}, f32[8,4,3,256]{3,2,1,0:T(4...) while((s32[]{:T(128)}, f32[192,2048]{1,0:T(8,128)S(1)}, ...), condition=%wide.region_8.9_spmd.clone, body=%wide.region_7.8_spmd.clone.sunk | while | flops 417072896 | bytes 4319797 | solution.py:102
  52.8 1.5 %gather_fusion = f32[4,3,256]{2,1,0:T(4,128)S(1)} fusion(f32[8,4,3,256]{3,2,1,0:T(4,128)} %get-tuple-element.539, s32[4]{0:T(128)S(1)} %get-tuple-element.507), kind=kCustom, calls=%fused_computation.clone.clone.1 | custom fusion | bytes 24608 | tf_op jit(solution)/shard_map/while/body/eval_jaxpr/gather | solution.py:91
  55.2 3.7 %convolution_add_fusion.2 = f32[192,2048]{1,0:T(8,128)S(1)} fusion(f32[2048]{0:T(1024)S(1)} %bitcast.130, f32[512]{0:T(512)S(1)} %bitcast.136, f32[2048]{0:T(1024)S(1)} %bitcast.131, f32[512]{0:T(512)S(1)} %bitcast.137, f32[2048]{0:T(1024)S(1)} %bitcast.129, f32[512]{0:T(512)S(1)} %bitcast.135, f32[192,2048]{1,0:T(8,128)S(1)} %get-tuple-element.526, ...), kind=kOutput, calls=%fused_computation.18.clone.1 | convolution fusion | flops 417071104 | bytes 3373057 | tf_op jit(solution)/shard_map/while/body/eval_jaxpr/dot_general | solution.py:98
  59.0 1.5 %gather_fusion = f32[4,3,256]{2,1,0:T(4,128)S(1)} fusion(f32[8,4,3,256]{3,2,1,0:T(4,128)} %get-tuple-element.539, s32[4]{0:T(128)S(1)} %get-tuple-element.507), kind=kCustom, calls=%fused_computation.clone.clone.1 | custom fusion | bytes 24608 | tf_op jit(solution)/shard_map/while/body/eval_jaxpr/gather | solution.py:91
  61.4 3.7 %convolution_add_fusion.2 = f32[192,2048]{1,0:T(8,128)S(1)} fusion(f32[2048]{0:T(1024)S(1)} %bitcast.130, f32[512]{0:T(512)S(1)} %bitcast.136, f32[2048]{0:T(1024)S(1)} %bitcast.131, f32[512]{0:T(512)S(1)} %bitcast.137, f32[2048]{0:T(1024)S(1)} %bitcast.129, f32[512]{0:T(512)S(1)} %bitcast.135, f32[192,2048]{1,0:T(8,128)S(1)} %get-tuple-element.526, ...), kind=kOutput, calls=%fused_computation.18.clone.1 | convolution fusion | flops 417071104 | bytes 3373057 | tf_op jit(solution)/shard_map/while/body/eval_jaxpr/dot_general | solution.py:98
  65.3 1.5 %gather_fusion = f32[4,3,256]{2,1,0:T(4,128)S(1)} fusion(f32[8,4,3,256]{3,2,1,0:T(4,128)} %get-tuple-element.539, s32[4]{0:T(128)S(1)} %get-tuple-element.507), kind=kCustom, calls=%fused_computation.clone.clone.1 | custom fusion | bytes 24608 | tf_op jit(solution)/shard_map/while/body/eval_jaxpr/gather | solution.py:91
  67.7 3.7 %convolution_add_fusion.2 = f32[192,2048]{1,0:T(8,128)S(1)} fusion(f32[2048]{0:T(1024)S(1)} %bitcast.130, f32[512]{0:T(512)S(1)} %bitcast.136, f32[2048]{0:T(1024)S(1)} %bitcast.131, f32[512]{0:T(512)S(1)} %bitcast.137, f32[2048]{0:T(1024)S(1)} %bitcast.129, f32[512]{0:T(512)S(1)} %bitcast.135, f32[192,2048]{1,0:T(8,128)S(1)} %get-tuple-element.526, ...), kind=kOutput, calls=%fused_computation.18.clone.1 | convolution fusion | flops 417071104 | bytes 3373057 | tf_op jit(solution)/shard_map/while/body/eval_jaxpr/dot_general | solution.py:98
  71.5 1.5 %gather_fusion = f32[4,3,256]{2,1,0:T(4,128)S(1)} fusion(f32[8,4,3,256]{3,2,1,0:T(4,128)} %get-tuple-element.539, s32[4]{0:T(128)S(1)} %get-tuple-element.507), kind=kCustom, calls=%fused_computation.clone.clone.1 | custom fusion | bytes 24608 | tf_op jit(solution)/shard_map/while/body/eval_jaxpr/gather | solution.py:91
  73.9 3.7 %convolution_add_fusion.2 = f32[192,2048]{1,0:T(8,128)S(1)} fusion(f32[2048]{0:T(1024)S(1)} %bitcast.130, f32[512]{0:T(512)S(1)} %bitcast.136, f32[2048]{0:T(1024)S(1)} %bitcast.131, f32[512]{0:T(512)S(1)} %bitcast.137, f32[2048]{0:T(1024)S(1)} %bitcast.129, f32[512]{0:T(512)S(1)} %bitcast.135, f32[192,2048]{1,0:T(8,128)S(1)} %get-tuple-element.526, ...), kind=kOutput, calls=%fused_computation.18.clone.1 | convolution fusion | flops 417071104 | bytes 3373057 | tf_op jit(solution)/shard_map/while/body/eval_jaxpr/dot_general | solution.py:98
  77.6 1.1 copy-done.2
  78.9 35.8 %while.32 = (s32[]{:T(128)}, f32[192,2048]{1,0:T(8,128)S(1)}, s32[2]{0:T(128)S(1)}, bf16[4,192,2048]{2,1,0:T(8,128)(2,1)}, f32[4,3,2048]{2,1,0:T(4,128)}, /*index=5*/f32[3,2048]{1,0:T(4,128)S(1)}, s32[]{:T(128)}) while((s32[]{:T(128)}, f32[192,2048]{1,0:T(8,128)S(1)}, s32[2]{0:T(128)S(1)}, bf16[4,192,2048]{2,1,0:T(8,128)(2,1)}, ...), condition=%wide.region_4.5_spmd, body=%wide.region_0.4_spmd.sunk | while | flops 1665531904 | bytes 4080315 | solution.py:64
  81.7 15.2 %conditional.2 = (f32[192,2048]{1,0:T(8,128)S(1)}) conditional(s32[]{:T(128)} %convert_element_type.63, f32[192,2048]{1,0:T(8,128)S(1)} %get-tuple-element.553, (s32[]{:T(128)}, bf16[4,192,2048]{2,1,0:T(8,128)(2,1)}, f32[4,3,2048]{2,1,0:T(4,128)}, f32[3,2048]{1,0:T(4,128)S(1)}, f32[192,2048]{1,0:T(8,128)S(1)}) %tuple.97), branch_computations={%region_2.2_spmd, %region_3.3_spmd} | conditional | flops 1665531904 | bytes 4080172 | solution.py:62
  81.7 0.9 constant_dynamic-slice_fusion.1
  82.7 14.3 %fusion.1 = f32[192,2048]{1,0:T(8,128)S(1)} fusion(f32[192,2048]{1,0:T(8,128)S(1)} %get-tuple-element.323, f32[2048]{0:T(1024)S(1)} %bitcast.133, f32[2048]{0:T(1024)S(1)} %bitcast.128, f32[2048]{0:T(1024)S(1)} %bitcast.134, f32[2048]{0:T(1024)S(1)} %bitcast.127, f32[2048]{0:T(1024)S(1)} %bitcast.132, f32[2048]{0:T(1024)S(1)} %bitcast.126, ...), kind=kOutput, calls=%fused_computation.6 | convolution fusion | flops 1665531904 | bytes 3981824 | tf_op jit(solution)/shard_map/while/body/eval_jaxpr/cond/branch_1_fun/dot_general | solution.py:55
  98.2 15.2 %conditional.2 = (f32[192,2048]{1,0:T(8,128)S(1)}) conditional(s32[]{:T(128)} %convert_element_type.63, f32[192,2048]{1,0:T(8,128)S(1)} %get-tuple-element.553, (s32[]{:T(128)}, bf16[4,192,2048]{2,1,0:T(8,128)(2,1)}, f32[4,3,2048]{2,1,0:T(4,128)}, f32[3,2048]{1,0:T(4,128)S(1)}, f32[192,2048]{1,0:T(8,128)S(1)}) %tuple.97), branch_computations={%region_2.2_spmd, %region_3.3_spmd} | conditional | flops 1665531904 | bytes 4080172 | solution.py:62
  98.2 0.9 constant_dynamic-slice_fusion.1
  99.2 14.3 %fusion.1 = f32[192,2048]{1,0:T(8,128)S(1)} fusion(f32[192,2048]{1,0:T(8,128)S(1)} %get-tuple-element.323, f32[2048]{0:T(1024)S(1)} %bitcast.133, f32[2048]{0:T(1024)S(1)} %bitcast.128, f32[2048]{0:T(1024)S(1)} %bitcast.134, f32[2048]{0:T(1024)S(1)} %bitcast.127, f32[2048]{0:T(1024)S(1)} %bitcast.132, f32[2048]{0:T(1024)S(1)} %bitcast.126, ...), kind=kOutput, calls=%fused_computation.6 | convolution fusion | flops 1665531904 | bytes 3981824 | tf_op jit(solution)/shard_map/while/body/eval_jaxpr/cond/branch_1_fun/dot_general | solution.py:55
  114.8 6.6 %fusion.39 = bf16[1,1,192,2048]{3,2,1,0:T(8,128)(2,1)} fusion(bf16[1,1,2048,2048]{3,2,1,0:T(8,128)(2,1)} %param.14, f32[192,2048]{1,0:T(8,128)} %copy-done.2, f32[192,2048]{1,0:T(8,128)S(1)} %get-tuple-element.344, bf16[1,1,192,2048]{3,2,1,0:T(8,128)(2,1)S(1)} %copy-done.3), kind=kOutput, calls=%fused_computation.65 | convolution fusion | flops 1612578816 | bytes 13107200 | tf_op jit(solution)/shard_map/dot_general | solution.py:104
  (109 shorter events, 10.1 us)
Async XLA Ops:
  6.5 7.6 %copy-start = (bf16[1,1,2048,256]{3,2,1,0:T(8,128)(2,1)S(1)}, bf16[1,1,2048,256]{3,2,1,0:T(8,128)(2,1)}, u32[]{:S(2)}) copy-start(bf16[1,1,2048,256]{3,2,1,0:T(8,128)(2,1)} %param.15) | copy-start | bytes 3145732
  14.1 26.8 %copy-start.1 = (bf16[192,2048]{1,0:T(8,128)(2,1)}, bf16[192,2048]{1,0:T(8,128)(2,1)S(1)}, u32[]{:S(2)}) copy-start(bf16[192,2048]{1,0:T(8,128)(2,1)S(1)} %fusion.33) | copy-start | bytes 2359300
  14.1 31.9 %copy-start.4 = (f32[1,4,3,2048]{3,1,2,0:T(4,128)S(1)}, f32[1,4,3,2048]{3,1,2,0:T(4,128)}, u32[]{:S(2)}) copy-start(f32[1,4,3,2048]{3,1,2,0:T(4,128)} %param.16) | copy-start | bytes 294916
  14.1 33.9 %copy-start.5 = (f32[8,4,3,256]{3,1,2,0:T(4,128)S(1)}, f32[8,4,3,256]{3,1,2,0:T(4,128)}, u32[]{:S(2)}) copy-start(f32[8,4,3,256]{3,1,2,0:T(4,128)} %param.17) | copy-start | bytes 294916
  16.1 19.0 %all-to-all-start = ((bf16[8,192,128]{2,1,0:T(8,128)(2,1)}), bf16[8,192,128]{2,1,0:T(8,128)(2,1)S(1)}, u32[]{:S(2)}, u32[]{:S(2)}) async-start(bf16[8,192,128]{2,1,0:T(8,128)(2,1)} %select_select_fusion), calls=%async_computation | async-start | bytes 786432 | tf_op jit(solution)/shard_map/all_to_all | solution.py:79
  23.4 54.2 %all-gather.3.cloned.1.call-start = ((), (), s32[]{:S(2)}) async-start(), calls=%async_computation.1 | async-start | bytes 3932160 | tf_op jit(solution)/shard_map/all_gather | solution.py:48
  35.7 5.1 %collective-permute-start = (bf16[4,192,128]{2,1,0:T(8,128)(2,1)S(1)}, bf16[4,192,128]{2,1,0:T(8,128)(2,1)S(1)}, u32[]{:S(2)}, u32[]{:S(2)}) collective-permute-start(bf16[4,192,128]{2,1,0:T(8,128)(2,1)S(1)} %broadcast_select_fusion), channel_id=1, source_target_pairs={{0,1},{1,2},{2,3},{3,0},{4,5},{5,6},{6,7},{7,4},{8,9},{9,10},{10,1... | collective-permute-start | bytes 589832 | tf_op jit(solution)/shard_map/ppermute | solution.py:16
  40.9 5.1 %collective-permute-start.1 = (bf16[4,192,128]{2,1,0:T(8,128)(2,1)S(1)}, bf16[4,192,128]{2,1,0:T(8,128)(2,1)S(1)}, u32[]{:S(2)}, u32[]{:S(2)}) collective-permute-start(bf16[4,192,128]{2,1,0:T(8,128)(2,1)S(1)} %collective-permute-done), channel_id=1, source_target_pairs={{0,1},{1,2},{2,3},{3,0},{4,5},{5,6},{6,7},{7,4},{8,9},{9,10},{10,1... | collective-permute-start | bytes 589832 | tf_op jit(solution)/shard_map/ppermute | solution.py:16
  46.0 6.1 %collective-permute-start.2 = (bf16[4,192,128]{2,1,0:T(8,128)(2,1)S(1)}, bf16[4,192,128]{2,1,0:T(8,128)(2,1)S(1)}, u32[]{:S(2)}, u32[]{:S(2)}) collective-permute-start(bf16[4,192,128]{2,1,0:T(8,128)(2,1)S(1)} %collective-permute-done.1), channel_id=1, source_target_pairs={{0,1},{1,2},{2,3},{3,0},{4,5},{5,6},{6,7},{7,4},{8,9},{9,10},{10,1... | collective-permute-start | bytes 589832 | tf_op jit(solution)/shard_map/ppermute | solution.py:16
  52.6 26.3 %copy-start.6 = (s32[1,1,2]{2,1,0:T(1,128)S(1)}, s32[1,1,2]{2,1,0:T(1,128)}, u32[]{:S(2)}) copy-start(s32[1,1,2]{2,1,0:T(1,128)} %param.18) | copy-start | bytes 28
  77.6 1.2 copy-start.2
  78.9 35.9 %copy-start.3 = (bf16[1,1,192,2048]{3,2,1,0:T(8,128)(2,1)S(1)}, bf16[1,1,192,2048]{3,2,1,0:T(8,128)(2,1)}, u32[]{:S(2)}) copy-start(bf16[1,1,192,2048]{3,2,1,0:T(8,128)(2,1)} %param.13) | copy-start | bytes 2359300
Sparse Core Ops, SparseCore 0:
  41.0 28.4 all-gather.2
